TPU v7x, 256 devices: a whole 4x4x8 slice. The times are simulated.
256 devices in a mesh: radial: 64 (over x, z, core), phi: 4 (over y).
Axes of the slice: x: 4, y: 4, z: 8, core: 2. Of those that a mesh axis runs over, the one named last changes fastest.
Arguments:
- conserved: float32 [8, 512, 64, 128], P(None, 'radial', 'phi'), may hold values from -2.5 to 7, as said below
- core_mass: float32 [1], replicated, may hold values from 0.2 to 1
Outputs:
- advanced: float32 [8, 512, 64, 128], P(None, 'radial', 'phi')
- enclosed_mass: float32 [512], P('radial')
Inputs may be any that keep to these rules, and one draw needn't show every extreme that they name: conserved[0] (density) lies between 0.4 and 2.5; conserved[4] exceeds (conserved[1]^2 + conserved[2]^2 + conserved[3]^2)/(2 conserved[0]) by at least 0.6; the speeds |conserved[m]/conserved[0]| stay below 1; conserved[5..7] lie between 0 and conserved[0].
All inputs are finite; a program needn't handle non-finite values.
Results may differ from a plain program's by a relative error of at most 0.0003.
Values sent between devices are 32-bit elements; how exact they have to be, the bound alone decides.
No kernel may reach another device: no remote copies, remote signals or barrier semaphores. Data moves between devices by JAX's collectives and lax.ppermute only.
A program may use at most 64 MiB of HBM per device.

v0:
```python
import math

import jax
import jax.numpy as jnp
from jax import lax
from jax.sharding import PartitionSpec as P

ADIABATIC = 4.0 / 3.0
INNER_RADIUS = 1.0
OUTER_RADIUS = 2.0
COURANT = 0.4
GRAVITY_KICK = 0.004
MINIMUM_DENSITY = 0.05
PRESSURE_FLOOR = 0.01


def from_everyone(value, axis):
    peers = lax.axis_size(axis)
    return lax.all_to_all(
        jnp.broadcast_to(value[None], (peers, *value.shape)), axis, 0, 0, tiled=True
    )


def taken_together(value, axis):
    return from_everyone(value, axis).sum(axis=0)


def combined_pairwise(pieces, combine):
    while len(jax.tree.leaves(pieces)[0]) > 1:
        pieces = jax.vmap(combine)(*(pieces[side::2] for side in (0, 1)))
    return pieces[0]


def entering(value, axis, combine, identity):
    peers, place = (lax.axis_size(axis), lax.axis_index(axis))
    passed = jnp.arange(peers) < place

    def kept(part, zero, own):
        part = jnp.where(
            passed.reshape(-1, *(1 for _ in own.shape)), part, jnp.asarray(zero, own.dtype)
        )
        return part

    pieces = from_everyone(value, axis)
    return combined_pairwise(kept(pieces, identity, value), combine)


def extended_2(value, sides, width, wrap):
    for axis, dim in sides:
        peers, length = (lax.axis_size(axis), value.shape[dim])
        up = [(i, (i + 1) % peers) for i in range(peers if wrap else peers - 1)]
        down = [(j, i) for i, j in up]
        last = lax.slice_in_dim(value, length - width, length, axis=dim)
        initial = lax.slice_in_dim(value, 0, width, axis=dim)
        before = lax.ppermute(last, axis, up)
        after = lax.ppermute(initial, axis, down)
        value = jnp.concatenate([before, value, after], axis=dim)
    return value


def step_sizes(radial_total, phi_total, theta_total):
    theta_step = math.pi / theta_total
    phi_step = 2.0 * math.pi / phi_total
    polar_width = INNER_RADIUS * math.sin(0.5 * theta_step) * phi_step
    radial_step = min(2.0 * polar_width, (OUTER_RADIUS - INNER_RADIUS) / radial_total)
    timestep = COURANT * min(radial_step, polar_width)
    return (radial_step, theta_step, phi_step, timestep)


def thermo(values):
    density = jnp.maximum(values[0], MINIMUM_DENSITY)
    kinetic = (
        0.5 * (values[1] * values[1] + values[2] * values[2] + values[3] * values[3]) / density
    )
    pressure = jnp.maximum((ADIABATIC - 1.0) * (values[4] - kinetic), PRESSURE_FLOOR * density)
    return (density, pressure)


def physical(values, component):
    density, pressure = thermo(values)
    normal = values[component] / density
    sound = jnp.sqrt(ADIABATIC * pressure / density)
    pieces = [values[which] * normal for which in range(values.shape[0])]
    pieces[component] = pieces[component] + pressure
    pieces[4] = pieces[4] + pressure * normal
    return (jnp.stack(pieces), jnp.abs(normal) + sound)


def face_flux(values, along_dim, component):
    interior = values.shape[along_dim] - 4
    neighbour_differences = lax.slice_in_dim(
        values, 1, interior + 4, axis=along_dim
    ) - lax.slice_in_dim(values, 0, interior + 3, axis=along_dim)
    below_diff = lax.slice_in_dim(neighbour_differences, 0, interior + 2, axis=along_dim)
    above_diff = lax.slice_in_dim(neighbour_differences, 1, interior + 3, axis=along_dim)
    limited = (
        0.5
        * (jnp.sign(below_diff) + jnp.sign(above_diff))
        * jnp.minimum(jnp.abs(below_diff), jnp.abs(above_diff))
    )
    left_state = lax.slice_in_dim(values, 1, interior + 2, axis=along_dim) + 0.5 * lax.slice_in_dim(
        limited, 0, interior + 1, axis=along_dim
    )
    right_state = lax.slice_in_dim(
        values, 2, interior + 3, axis=along_dim
    ) - 0.5 * lax.slice_in_dim(limited, 1, interior + 2, axis=along_dim)
    left_flux, left_signal = physical(left_state, component)
    right_flux, right_signal = physical(right_state, component)
    signal = jnp.maximum(left_signal, right_signal)
    return 0.5 * (left_flux + right_flux) - 0.5 * signal * (right_state - left_state)


def hydro_rate(extended, cell_centers, enclosed, radial_step, theta_step, phi_step, strength):
    theta_cells = extended.shape[3]
    centre_cells = extended[:, 2:-2, 2:-2, :]
    polar_padded = jnp.pad(centre_cells, ((0, 0), (0, 0), (0, 0), (2, 2)), mode="edge")
    radial_flux = face_flux(extended[:, :, 2:-2, :], 1, 1)
    polar_flux = face_flux(polar_padded, 3, 2)
    azimuth_flux = face_flux(extended[:, 2:-2, :, :], 2, 3)
    angles = (jnp.arange(theta_cells, dtype=jnp.float32) + 0.5) * theta_step
    sine_center = jnp.sin(angles)
    cosine = jnp.cos(angles)
    face_sine = jnp.sin(jnp.arange(theta_cells + 1, dtype=jnp.float32) * theta_step)
    radius = cell_centers[:, None, None]
    face_radius = jnp.concatenate(
        [cell_centers - 0.5 * radial_step, cell_centers[-1:] + 0.5 * radial_step]
    )[:, None, None]
    radial_area = face_radius * face_radius * radial_flux
    divergence = (radial_area[:, 1:] - radial_area[:, :-1]) / (radius * radius * radial_step)
    polar_area = face_sine * polar_flux
    divergence = divergence + (polar_area[..., 1:] - polar_area[..., :-1]) / (
        radius * sine_center * theta_step
    )
    divergence = divergence + (azimuth_flux[:, :, 1:] - azimuth_flux[:, :, :-1]) / (
        radius * sine_center * phi_step
    )
    density, pressure = thermo(centre_cells)
    radial_speed = centre_cells[1] / density
    polar_speed = centre_cells[2] / density
    azimuth_speed = centre_cells[3] / density
    cotangent = cosine / sine_center
    gravity_pull = strength * enclosed[:, None, None] / (radius * radius)
    source_radial = (
        2.0 * pressure + density * (polar_speed * polar_speed + azimuth_speed * azimuth_speed)
    ) / radius - density * gravity_pull
    source_polar = (
        pressure * cotangent
        + density * azimuth_speed * azimuth_speed * cotangent
        - density * radial_speed * polar_speed
    ) / radius
    source_azimuth = -density * azimuth_speed * (radial_speed + polar_speed * cotangent) / radius
    source_energy = -centre_cells[1] * gravity_pull
    nothing = jnp.zeros_like(pressure)
    source = jnp.stack(
        [
            nothing,
            source_radial,
            source_polar,
            source_azimuth,
            source_energy,
            nothing,
            nothing,
            nothing,
        ]
    )
    return source - divergence


def add_terms(earlier, later):
    return earlier + later


def body(conserved, core_mass):
    radial_rows = conserved.shape[1]
    phi_cells = conserved.shape[2]
    theta_cells = conserved.shape[3]
    radial_devices = lax.axis_size("radial")
    position = lax.axis_index("radial")
    radial_step, theta_step, phi_step, timestep = step_sizes(
        radial_rows * radial_devices, phi_cells * lax.axis_size("phi"), theta_cells
    )
    strength = GRAVITY_KICK / timestep
    first_row = position * radial_rows
    cell_centers = (
        INNER_RADIUS
        + ((first_row + jnp.arange(radial_rows, dtype=jnp.int32)).astype(jnp.float32) + 0.5)
        * radial_step
    )
    sine_center = jnp.sin((jnp.arange(theta_cells, dtype=jnp.float32) + 0.5) * theta_step)
    local_shells = jnp.dot(
        jnp.sum(conserved[0], axis=1), sine_center, precision=lax.Precision.HIGHEST
    )
    local_shells = (
        local_shells * cell_centers * cell_centers * (radial_step * theta_step * phi_step)
    )
    shells = taken_together(local_shells, "phi")
    before = entering(jnp.sum(shells), "radial", add_terms, jnp.float32(0.0))
    enclosed = core_mass[0] + before + jnp.cumsum(shells) - 0.5 * shells

    def clipped_rows(extended, halo_width):
        total_rows = extended.shape[1]
        low_rows = jnp.where(
            position == 0,
            lax.slice_in_dim(extended, halo_width, halo_width + 1, axis=1),
            lax.slice_in_dim(extended, 0, halo_width, axis=1),
        )
        high_rows = jnp.where(
            position == radial_devices - 1,
            lax.slice_in_dim(
                extended, total_rows - halo_width - 1, total_rows - halo_width, axis=1
            ),
            lax.slice_in_dim(extended, total_rows - halo_width, total_rows, axis=1),
        )
        middle = lax.slice_in_dim(extended, halo_width, total_rows - halo_width, axis=1)
        return jnp.concatenate([low_rows, middle, high_rows], axis=1)

    def extend(values):
        wedge_split_state = extended_2(values, (("phi", 2),), 2, True)
        slab_split_state = extended_2(wedge_split_state, (("radial", 1),), 2, False)
        return clipped_rows(slab_split_state, 2)

    section_one = conserved + timestep * hydro_rate(
        extend(conserved), cell_centers, enclosed, radial_step, theta_step, phi_step, strength
    )
    section_two = section_one + timestep * hydro_rate(
        extend(section_one), cell_centers, enclosed, radial_step, theta_step, phi_step, strength
    )
    advanced = 0.5 * conserved + 0.5 * section_two
    return (advanced, enclosed)


def solution(mesh):
    in_specs = (P(None, "radial", "phi", None), P())
    out_specs = (P(None, "radial", "phi", None), P("radial"))
    return jax.shard_map(body, mesh=mesh, in_specs=in_specs, out_specs=out_specs, check_vma=False)
```

profile of v0, /device:TPU:2, one launch (start us, length us, event | category | flops | bytes accessed | tf_op | source)
XLA Modules:
  0.0 79.3 jit_solution(11763445968841728372)
XLA Ops:
  0.6 1.1 %fusion.54 = (f32[8,8,2,128]{3,2,1,0:T(2,128)S(1)}, f32[8,8,2,128]{3,2,1,0:T(2,128)S(1)}) fusion(f32[8,8,16,128]{3,2,1,0:T(8,128)} %param.2), kind=kLoop, calls=%fused_computation.340 | loop fusion | bytes 262144 | tf_op jit(solution)/shard_map/slice | solution.py:53
  1.8 1.7 %collective-permute-start = (f32[8,8,2,128]{3,1,2,0:T(8,128)S(1)}, f32[8,8,2,128]{3,1,2,0:T(8,128)S(1)}, u32[]{:S(2)}, u32[]{:S(2)}) collective-permute-start(f32[8,8,2,128]{3,1,2,0:T(8,128)S(1)} %copy.721), channel_id=1, source_target_pairs={{0,1},{1,2},{2,3},{3,0},{4,5},{5,6},{6,7},{7,4},{8,9},{9,10},{10,1... | collective-permute-start | bytes 196616 | tf_op jit(solution)/shard_map/ppermute | solution.py:55
  3.5 1.7 %collective-permute-start.1 = (f32[8,8,2,128]{3,1,2,0:T(8,128)S(1)}, f32[8,8,2,128]{3,1,2,0:T(8,128)S(1)}, u32[]{:S(2)}, u32[]{:S(2)}) collective-permute-start(f32[8,8,2,128]{3,1,2,0:T(8,128)S(1)} %copy.722), channel_id=1, source_target_pairs={{1,0},{2,1},{3,2},{0,3},{5,4},{6,5},{7,6},{4,7},{9,8},{10,9},{11,1... | collective-permute-start | bytes 196616 | tf_op jit(solution)/shard_map/ppermute | solution.py:56
  5.1 0.9 %slice_reduce_fusion.2 = f32[8,128]{1,0:T(8,128)S(1)} fusion(f32[8,8,16,128]{3,2,1,0:T(8,128)} %param.2), kind=kLoop, calls=%fused_computation.312 | loop fusion | flops 15360 | bytes 69632
  6.1 0.6 broadcast_in_dim.45
  6.7 3.3 %all-to-all-start = ((f32[4,1,8]{2,1,0:T(1,128)}), f32[4,1,8]{2,1,0:T(1,128)S(1)}, u32[]{:S(2)}, u32[]{:S(2)}) async-start(f32[4,1,8]{2,1,0:T(1,128)} %broadcast_in_dim.45), calls=%async_computation | async-start | bytes 4096 | tf_op jit(solution)/shard_map/all_to_all | solution.py:19
  10.4 0.6 slice.760
  11.0 0.4 copy.723
  11.4 0.4 copy.724
  11.9 0.2 reshape.178
  12.3 0.5 pad_maximum_fusion.6
  12.8 0.3 slice_subtract_fusion.1
  13.1 0.7 minimum_multiply_fusion.1
  13.9 0.8 fusion.6
  14.6 0.2 multiply_bitcast_fusion.1
  16.1 0.5 subtract_multiply_fusion.1
  16.7 0.6 fusion.48
  17.3 1.3 %broadcast_in_dim.46 = f32[64,1,1]{2,1,0:T(1,128)} broadcast(f32[]{:T(128)} %get-tuple-element.18), dimensions={} | broadcast | bytes 260 | tf_op jit(solution)/shard_map/broadcast_in_dim | solution.py:20
  18.6 12.0 %all-to-all-start.1 = ((f32[64,1,1]{2,1,0:T(1,128)}), f32[64,1,1]{2,1,0:T(1,128)S(1)}, u32[]{:S(2)}, u32[]{:S(2)}) async-start(f32[64,1,1]{2,1,0:T(1,128)} %broadcast_in_dim.46), calls=%async_computation.1 | async-start | bytes 65536 | tf_op jit(solution)/shard_map/all_to_all | solution.py:19
  31.4 7.7 %all-to-all-done.1 = f32[64,1,1]{2,1,0:T(1,128)S(1)} async-done(((f32[64,1,1]{2,1,0:T(1,128)}), f32[64,1,1]{2,1,0:T(1,128)S(1)}, u32[]{:S(2)}, u32[]{:S(2)}) %all-to-all-start.1) | async-done | bytes 288 | tf_op jit(solution)/shard_map/all_to_all | solution.py:19
  39.1 0.6 reduce.4
  40.8 0.6 fusion.55
  42.7 0.5 multiply_divide_fusion
  44.0 2.8 %collective-permute-start.3 = (f32[8,2,20,128]{3,0,2,1:T(8,128)S(1)}, f32[8,2,20,128]{3,0,2,1:T(8,128)S(1)}, u32[]{:S(2)}, u32[]{:S(2)}) collective-permute-start(f32[8,2,20,128]{3,0,2,1:T(8,128)S(1)} %copy.686), channel_id=1, source_target_pairs={{4,0},{8,4},{12,8},{16,12},{20,16},{24,20},{28,24},{32,28},{36,32}... | collective-permute-start | bytes 491528 | tf_op jit(solution)/shard_map/ppermute | solution.py:56
  46.9 2.1 %collective-permute-start.2 = (f32[8,2,20,128]{3,0,2,1:T(8,128)S(1)}, f32[8,2,20,128]{3,0,2,1:T(8,128)S(1)}, u32[]{:S(2)}, u32[]{:S(2)}) collective-permute-start(f32[8,2,20,128]{3,0,2,1:T(8,128)S(1)} %copy.682), channel_id=1, source_target_pairs={{0,4},{4,8},{8,12},{12,16},{16,20},{20,24},{24,28},{28,32},{32,36}... | collective-permute-start | bytes 491528 | tf_op jit(solution)/shard_map/ppermute | solution.py:55
  49.0 0.6 minimum_multiply_fusion.3
  49.5 0.3 fusion.10
  50.7 4.9 %collective-permute-done.2 = f32[8,2,20,128]{3,0,2,1:T(8,128)S(1)} collective-permute-done((f32[8,2,20,128]{3,0,2,1:T(8,128)S(1)}, f32[8,2,20,128]{3,0,2,1:T(8,128)S(1)}, u32[]{:S(2)}, u32[]{:S(2)}) %collective-permute-start.2) | collective-permute-done | bytes 163872 | tf_op jit(solution)/shard_map/ppermute | solution.py:55
  55.9 0.3 minimum_multiply_fusion.5
  57.0 0.4 fusion.28
  57.4 0.5 slice_reduce_fusion.1
  57.9 2.1 %collective-permute-start.4 = (f32[8,8,2,128]{3,1,2,0:T(8,128)S(1)}, f32[8,8,2,128]{3,1,2,0:T(8,128)S(1)}, u32[]{:S(2)}, u32[]{:S(2)}) collective-permute-start(f32[8,8,2,128]{3,1,2,0:T(8,128)S(1)} %copy.696), channel_id=1, source_target_pairs={{0,1},{1,2},{2,3},{3,0},{4,5},{5,6},{6,7},{7,4},{8,9},{9,10},{10,1... | collective-permute-start | bytes 196616 | tf_op jit(solution)/shard_map/ppermute | solution.py:55
  60.0 1.3 %collective-permute-start.5 = (f32[8,8,2,128]{3,1,2,0:T(8,128)S(1)}, f32[8,8,2,128]{3,1,2,0:T(8,128)S(1)}, u32[]{:S(2)}, u32[]{:S(2)}) collective-permute-start(f32[8,8,2,128]{3,1,2,0:T(8,128)S(1)} %copy.697), channel_id=1, source_target_pairs={{1,0},{2,1},{3,2},{0,3},{5,4},{6,5},{7,6},{4,7},{9,8},{10,9},{11,1... | collective-permute-start | bytes 196616 | tf_op jit(solution)/shard_map/ppermute | solution.py:56
  61.7 0.5 pad_maximum_fusion.7
  62.2 0.3 slice_subtract_fusion
  62.6 0.7 minimum_multiply_fusion
  63.3 0.7 fusion.4
  64.1 0.2 multiply_bitcast_fusion
  65.1 0.5 subtract_multiply_fusion
  66.1 1.9 %collective-permute-start.6 = (f32[8,2,20,128]{3,0,2,1:T(8,128)S(1)}, f32[8,2,20,128]{3,0,2,1:T(8,128)S(1)}, u32[]{:S(2)}, u32[]{:S(2)}) collective-permute-start(f32[8,2,20,128]{3,0,2,1:T(8,128)S(1)} %copy.702), channel_id=1, source_target_pairs={{0,4},{4,8},{8,12},{12,16},{16,20},{20,24},{24,28},{28,32},{32,36}... | collective-permute-start | bytes 491528 | tf_op jit(solution)/shard_map/ppermute | solution.py:55
  68.1 6.0 %collective-permute-start.7 = (f32[8,2,20,128]{3,0,2,1:T(8,128)S(1)}, f32[8,2,20,128]{3,0,2,1:T(8,128)S(1)}, u32[]{:S(2)}, u32[]{:S(2)}) collective-permute-start(f32[8,2,20,128]{3,0,2,1:T(8,128)S(1)} %copy.706), channel_id=1, source_target_pairs={{4,0},{8,4},{12,8},{16,12},{20,16},{24,20},{28,24},{32,28},{36,32}... | collective-permute-start | bytes 491528 | tf_op jit(solution)/shard_map/ppermute | solution.py:56
  74.1 0.6 minimum_multiply_fusion.2
  74.7 0.3 fusion.8
  75.5 0.2 multiply_subtract_fusion
  75.9 0.8 %collective-permute-done.7 = f32[8,2,20,128]{3,0,2,1:T(8,128)S(1)} collective-permute-done((f32[8,2,20,128]{3,0,2,1:T(8,128)S(1)}, f32[8,2,20,128]{3,0,2,1:T(8,128)S(1)}, u32[]{:S(2)}, u32[]{:S(2)}) %collective-permute-start.7) | collective-permute-done | bytes 163872 | tf_op jit(solution)/shard_map/ppermute | solution.py:56
  77.0 0.3 minimum_multiply_fusion.4
  77.9 0.2 subtract_multiply_fusion.2
  78.1 1.2 %fusion.32 = f32[8,8,16,128]{3,2,1,0:T(8,128)} fusion(f32[8,8,16,128]{3,2,1,0:T(8,128)S(1)} %copy-done, f32[8,8,16,128]{3,2,1,0:T(8,128)S(1)} %fusion.28, f32[8,8,16,128]{3,2,1,0:T(8,128)S(1)} %constant_dynamic-update-slice_fusion.55, f32[8,8,17,128]{3,2,1,0:T(8,128)S(1)} %multiply_subtract_fusion, f32[8,8,16,129]{3,2,1,0:T(8,128)S(1)} %subtract_multiply_fusion, ...), kind=kLoop, calls=%fused_computation.97 | loop fusion | flops 1703936 | bytes 5251104 | tf_op jit(solution)/shard_map/add | solution.py:228
  (182 shorter events, 7.9 us)
Async XLA Ops:
  0.6 9.4 %copy-start = (f32[8,8,16,128]{3,2,1,0:T(8,128)S(1)}, f32[8,8,16,128]{3,2,1,0:T(8,128)}, u32[]{:S(2)}) copy-start(f32[8,8,16,128]{3,2,1,0:T(8,128)} %param.2) | copy-start | bytes 1572868
  1.8 41.8 %collective-permute-start = (f32[8,8,2,128]{3,1,2,0:T(8,128)S(1)}, f32[8,8,2,128]{3,1,2,0:T(8,128)S(1)}, u32[]{:S(2)}, u32[]{:S(2)}) collective-permute-start(f32[8,8,2,128]{3,1,2,0:T(8,128)S(1)} %copy.721), channel_id=1, source_target_pairs={{0,1},{1,2},{2,3},{3,0},{4,5},{5,6},{6,7},{7,4},{8,9},{9,10},{10,1... | collective-permute-start | bytes 196616 | tf_op jit(solution)/shard_map/ppermute | solution.py:55
  3.5 40.2 %collective-permute-start.1 = (f32[8,8,2,128]{3,1,2,0:T(8,128)S(1)}, f32[8,8,2,128]{3,1,2,0:T(8,128)S(1)}, u32[]{:S(2)}, u32[]{:S(2)}) collective-permute-start(f32[8,8,2,128]{3,1,2,0:T(8,128)S(1)} %copy.722), channel_id=1, source_target_pairs={{1,0},{2,1},{3,2},{0,3},{5,4},{6,5},{7,6},{4,7},{9,8},{10,9},{11,1... | collective-permute-start | bytes 196616 | tf_op jit(solution)/shard_map/ppermute | solution.py:56
  6.7 9.9 %all-to-all-start = ((f32[4,1,8]{2,1,0:T(1,128)}), f32[4,1,8]{2,1,0:T(1,128)S(1)}, u32[]{:S(2)}, u32[]{:S(2)}) async-start(f32[4,1,8]{2,1,0:T(1,128)} %broadcast_in_dim.45), calls=%async_computation | async-start | bytes 4096 | tf_op jit(solution)/shard_map/all_to_all | solution.py:19
  18.6 20.6 %all-to-all-start.1 = ((f32[64,1,1]{2,1,0:T(1,128)}), f32[64,1,1]{2,1,0:T(1,128)S(1)}, u32[]{:S(2)}, u32[]{:S(2)}) async-start(f32[64,1,1]{2,1,0:T(1,128)} %broadcast_in_dim.46), calls=%async_computation.1 | async-start | bytes 65536 | tf_op jit(solution)/shard_map/all_to_all | solution.py:19
  44.0 6.6 %collective-permute-start.3 = (f32[8,2,20,128]{3,0,2,1:T(8,128)S(1)}, f32[8,2,20,128]{3,0,2,1:T(8,128)S(1)}, u32[]{:S(2)}, u32[]{:S(2)}) collective-permute-start(f32[8,2,20,128]{3,0,2,1:T(8,128)S(1)} %copy.686), channel_id=1, source_target_pairs={{4,0},{8,4},{12,8},{16,12},{20,16},{24,20},{28,24},{32,28},{36,32}... | collective-permute-start | bytes 491528 | tf_op jit(solution)/shard_map/ppermute | solution.py:56
  46.9 8.7 %collective-permute-start.2 = (f32[8,2,20,128]{3,0,2,1:T(8,128)S(1)}, f32[8,2,20,128]{3,0,2,1:T(8,128)S(1)}, u32[]{:S(2)}, u32[]{:S(2)}) collective-permute-start(f32[8,2,20,128]{3,0,2,1:T(8,128)S(1)} %copy.682), channel_id=1, source_target_pairs={{0,4},{4,8},{8,12},{12,16},{16,20},{20,24},{24,28},{28,32},{32,36}... | collective-permute-start | bytes 491528 | tf_op jit(solution)/shard_map/ppermute | solution.py:55
  57.9 7.8 %collective-permute-start.4 = (f32[8,8,2,128]{3,1,2,0:T(8,128)S(1)}, f32[8,8,2,128]{3,1,2,0:T(8,128)S(1)}, u32[]{:S(2)}, u32[]{:S(2)}) collective-permute-start(f32[8,8,2,128]{3,1,2,0:T(8,128)S(1)} %copy.696), channel_id=1, source_target_pairs={{0,1},{1,2},{2,3},{3,0},{4,5},{5,6},{6,7},{7,4},{8,9},{9,10},{10,1... | collective-permute-start | bytes 196616 | tf_op jit(solution)/shard_map/ppermute | solution.py:55
  60.0 5.7 %collective-permute-start.5 = (f32[8,8,2,128]{3,1,2,0:T(8,128)S(1)}, f32[8,8,2,128]{3,1,2,0:T(8,128)S(1)}, u32[]{:S(2)}, u32[]{:S(2)}) collective-permute-start(f32[8,8,2,128]{3,1,2,0:T(8,128)S(1)} %copy.697), channel_id=1, source_target_pairs={{1,0},{2,1},{3,2},{0,3},{5,4},{6,5},{7,6},{4,7},{9,8},{10,9},{11,1... | collective-permute-start | bytes 196616 | tf_op jit(solution)/shard_map/ppermute | solution.py:56
  66.1 9.7 %collective-permute-start.6 = (f32[8,2,20,128]{3,0,2,1:T(8,128)S(1)}, f32[8,2,20,128]{3,0,2,1:T(8,128)S(1)}, u32[]{:S(2)}, u32[]{:S(2)}) collective-permute-start(f32[8,2,20,128]{3,0,2,1:T(8,128)S(1)} %copy.702), channel_id=1, source_target_pairs={{0,4},{4,8},{8,12},{12,16},{16,20},{20,24},{24,28},{28,32},{32,36}... | collective-permute-start | bytes 491528 | tf_op jit(solution)/shard_map/ppermute | solution.py:55
  68.1 8.6 %collective-permute-start.7 = (f32[8,2,20,128]{3,0,2,1:T(8,128)S(1)}, f32[8,2,20,128]{3,0,2,1:T(8,128)S(1)}, u32[]{:S(2)}, u32[]{:S(2)}) collective-permute-start(f32[8,2,20,128]{3,0,2,1:T(8,128)S(1)} %copy.706), channel_id=1, source_target_pairs={{4,0},{8,4},{12,8},{16,12},{20,16},{24,20},{28,24},{32,28},{36,32}... | collective-permute-start | bytes 491528 | tf_op jit(solution)/shard_map/ppermute | solution.py:56
where the time goes:
time: 79.7 us; the launch traced here: 79.3 us
  starting transfers between devices  34.8 us (44%)
  other arithmetic  18.4 us (23%)
  waiting for transfers between devices  13.5 us (17%)
  local copies, waits for them, and re-layouts  8.12 us (10%)
  between operations  4.41 us (6%)
    all_to_all x2, starting transfers between devices, from_everyone(): lax.all_to_all(jnp.broadcast_to(value[None], (peers, *value.shape)), axis...  15.3 us
    ppermute x4, starting transfers between devices, extended_2(): after = lax.ppermute(initial, axis, down)  11.7 us
    ppermute x4, starting transfers between devices, extended_2(): before = lax.ppermute(last, axis, up)  7.77 us
    all_to_all x2, waiting for transfers between devices, from_everyone(): lax.all_to_all(jnp.broadcast_to(value[None], (peers, *value.shape)), axis...  7.71 us
    ppermute x4, waiting for transfers between devices, extended_2(): before = lax.ppermute(last, axis, up)  4.95 us
    mul x6, other arithmetic, face_flux(): 0.5 * (jnp.sign(below_diff) + jnp.sign(above_diff))  3.14 us
    unnamed x93, other arithmetic  3.07 us
    add x6, other arithmetic, face_flux(): lax.slice_in_dim(values, 1, interior + 2, axis=along_dim)  2.36 us
  transfers between devices with their start and end apart: 10, of which 3 were waited for; matrix products, arithmetic and copies ran while one was open for 25% of the time, Pallas kernels for 0%

commit v1 on v0

v1 whole, which is shorter than its diff:
```python
import math

import jax
import jax.numpy as jnp
import numpy as np
from jax import lax
from jax.experimental import pallas as pl
from jax.experimental.pallas import tpu as pltpu
from jax.sharding import PartitionSpec as P

ADIABATIC = 4.0 / 3.0
INNER_RADIUS = 1.0
OUTER_RADIUS = 2.0
COURANT = 0.4
GRAVITY_KICK = 0.004
MINIMUM_DENSITY = 0.05
PRESSURE_FLOOR = 0.01
NV = 8
LANES = 128
VMEM_LIMIT = 12 * 1024 * 1024


def step_sizes(radial_total, phi_total, theta_total):
    theta_step = math.pi / theta_total
    phi_step = 2.0 * math.pi / phi_total
    polar_width = INNER_RADIUS * math.sin(0.5 * theta_step) * phi_step
    radial_step = min(2.0 * polar_width, (OUTER_RADIUS - INNER_RADIUS) / radial_total)
    timestep = COURANT * min(radial_step, polar_width)
    return (radial_step, theta_step, phi_step, timestep)


def angle_table(theta_cells, theta_step, phi_step):
    angles = (np.arange(theta_cells, dtype=np.float32) + np.float32(0.5)) * np.float32(theta_step)
    sine, cosine = np.sin(angles), np.cos(angles)
    faces = np.sin(np.arange(theta_cells + 1, dtype=np.float32) * np.float32(theta_step))
    rows = [sine, cosine / sine, faces[1:], faces[:-1], 1.0 / (sine * theta_step), 1.0 / (sine * phi_step)]
    table = np.zeros((8, theta_cells), np.float32)
    for k, row in enumerate(rows):
        table[k] = row
    return table


def half_slope(below, above):
    return jnp.maximum(jnp.minimum(below, above), 0.0) + jnp.minimum(jnp.maximum(below, above), 0.0)


def thermo(u):
    density = jnp.maximum(u[0], MINIMUM_DENSITY)
    inverse = 1.0 / density
    kinetic = 0.5 * (u[1] * u[1] + u[2] * u[2] + u[3] * u[3]) * inverse
    pressure = jnp.maximum((ADIABATIC - 1.0) * (u[4] - kinetic), PRESSURE_FLOOR * density)
    return density, inverse, pressure


def side(u, component):
    _, inverse, pressure = thermo(u)
    normal = u[component] * inverse
    sound = jnp.sqrt((ADIABATIC * pressure) * inverse)
    return normal, pressure, jnp.abs(normal) + sound


def face_flux(left, right, component):
    vl, pl_, al = side(left, component)
    vr, pr, ar = side(right, component)
    signal = jnp.maximum(al, ar)
    out = []
    for k in range(NV):
        if k == 4:
            total = (left[k] + pl_) * vl + (right[k] + pr) * vr
        else:
            total = left[k] * vl + right[k] * vr
        if k == component:
            total = total + (pl_ + pr)
        out.append(total - signal * (right[k] - left[k]))
    return out


def rate_rows(x, radial_flux, left_row, table, rows, wide, first_row, steps, emit):
    radial_step = steps[0]
    ring = x.shape[2]

    def radius_of(index):
        return INNER_RADIUS + (jnp.full((1, LANES), index, jnp.float32) + 0.5) * radial_step

    def states(j):
        left, right = [], []
        for k in range(NV):
            centre = x[k, j, :wide]
            slope = half_slope(0.5 * (centre - x[k, j - 1, :wide]), 0.5 * (x[k, j + 1, :wide] - centre))
            left.append(centre + slope)
            right.append(centre - slope)
        return left, right

    left, _ = states(1)
    for k in range(NV):
        left_row[k] = left[k]

    def radial_face(f, carry):
        above, right = states(f + 2)
        flux = face_flux([left_row[k] for k in range(NV)], right, 1)
        face = radius_of((first_row + f).astype(jnp.float32)) - 0.5 * radial_step
        area = 0.5 * face * face
        for k in range(NV):
            radial_flux[f, k] = area * flux[k]
            left_row[k] = above[k]
        return carry

    lax.fori_loop(0, rows + 1, radial_face, 0)

    last = lax.broadcasted_iota(jnp.int32, (wide, LANES), 1) == LANES - 1

    def row(r, carry):
        radius = radius_of((first_row + r).astype(jnp.float32))
        inverse_radius = 1.0 / radius
        radial_scale = inverse_radius * inverse_radius * (1.0 / radial_step)
        u = [x[k, r + 2, :wide] for k in range(NV)]
        rate = []
        for k in range(NV):
            rate.append((radial_flux[r, k] - radial_flux[r + 1, k]) * radial_scale)
        left, right = [], []
        for k in range(NV):
            above = jnp.where(last, 0.0, 0.5 * (pltpu.roll(u[k], LANES - 1, 1) - u[k]))
            below = pltpu.roll(above, 1, 1)
            slope = half_slope(below, above)
            left.append(u[k] + slope)
            right.append(jnp.where(last, u[k], pltpu.roll(u[k] - slope, LANES - 1, 1)))
        flux = face_flux(left, right, 2)
        polar_scale = table[4:5, :] * (0.5 * inverse_radius)
        upper, lower = table[2:3, :] * polar_scale, table[3:4, :] * polar_scale
        for k in range(NV):
            rate[k] = rate[k] - (upper * flux[k] - lower * pltpu.roll(flux[k], 1, 1))
        left, right = [], []
        for k in range(NV):
            ext = x[k, r + 2]
            above = 0.5 * (pltpu.roll(ext, ring - 1, 0) - ext)
            below = pltpu.roll(above, 1, 0)
            slope = half_slope(below, above)
            left.append(ext + slope)
            right.append(pltpu.roll(ext - slope, ring - 1, 0))
        flux = face_flux(left, right, 3)
        azimuth_scale = table[5:6, :] * (0.5 * inverse_radius)
        for k in range(NV):
            rate[k] = rate[k] - azimuth_scale * (flux[k][:wide] - pltpu.roll(flux[k], 1, 0)[:wide])
        density, inverse, pressure = thermo(u)
        cotangent = table[1:2, :]
        vr, vt, vp = u[1] * inverse, u[2] * inverse, u[3] * inverse
        azimuth_push = density * vp * vp
        rate[1] = rate[1] + (2.0 * pressure + (density * vt * vt + azimuth_push)) * inverse_radius
        rate[2] = rate[2] + ((pressure + azimuth_push) * cotangent - density * vr * vt) * inverse_radius
        rate[3] = rate[3] - density * vp * (vr + vt * cotangent) * inverse_radius
        emit(r, u, rate)
        return carry

    lax.fori_loop(0, rows, row, 0)


def fill_ends(x, rows, position, last_position):
    first = (x.shape[1] - rows) // 2
    last = first + rows - 1

    @pl.when(position == 0)
    def _():
        for k in range(NV):
            x[k, first - 2] = x[k, first]
            x[k, first - 1] = x[k, first]

    @pl.when(position == last_position)
    def _():
        for k in range(NV):
            x[k, last + 1] = x[k, last]
            x[k, last + 2] = x[k, last]


def solution(mesh):
    radial_devices, phi_devices = mesh.shape["radial"], mesh.shape["phi"]
    assert phi_devices == 4
    up = [(i, (i + 1) % radial_devices) for i in range(radial_devices)]
    down = [(j, i) for i, j in up]
    clockwise = [(i, (i + 1) % phi_devices) for i in range(phi_devices)]
    counter = [(j, i) for i, j in clockwise]
    opposite = [(i, (i + 2) % phi_devices) for i in range(phi_devices)]

    def body(conserved, core_mass):
        _, rows, wedge, theta_cells = conserved.shape
        steps = step_sizes(rows * radial_devices, wedge * phi_devices, theta_cells)
        radial_step, theta_step, phi_step, timestep = steps
        strength = GRAVITY_KICK / timestep
        ring, outer = wedge + 8, rows + 4
        table = jnp.asarray(angle_table(theta_cells, theta_step, phi_step))
        position = lax.axis_index("radial").astype(jnp.int32).reshape(1)
        smem = pl.BlockSpec(memory_space=pltpu.SMEM)
        vmem = pl.BlockSpec(memory_space=pltpu.VMEM)
        f32 = jnp.float32
        limit = pltpu.CompilerParams(vmem_limit_bytes=VMEM_LIMIT)

        def shape(*sizes):
            return jax.ShapeDtypeStruct(sizes, f32)

        def radius_at(index):
            return INNER_RADIUS + (jnp.full((1, LANES), index, f32) + 0.5) * radial_step

        side_rows = NV * rows * 4

        def pack(where, u, angles, mass, before, after):
            lane = lax.broadcasted_iota(jnp.int32, (1, LANES), 1)
            line = jnp.zeros((1, LANES), f32)
            for r in range(rows):
                radius = radius_at((where[0] * rows + r).astype(f32))
                total = jnp.sum(u[0, r] * angles[0:1, :], axis=(0, 1), keepdims=True)
                shell = total * (radius * radius * (radial_step * theta_step * phi_step))
                line = jnp.where(lane == r, shell, line)
            tile = jnp.broadcast_to(line, (8, LANES))
            mass[...] = tile
            for target, start in ((before, 0), (after, wedge - 4)):
                target[side_rows : side_rows + 8] = tile
                for k in range(NV):
                    for r in range(rows):
                        at = (k * rows + r) * 4
                        target[at : at + 4] = u[k, r, start : start + 4]

        mass, wedge_before, wedge_after = pl.pallas_call(
            pack,
            out_shape=[shape(8, LANES), shape(side_rows + 8, LANES), shape(side_rows + 8, LANES)],
            in_specs=[smem, vmem, vmem],
            out_specs=[vmem] * 3,
            compiler_params=limit,
            name="pack",
        )(position, conserved, table)

        wedge_low = lax.ppermute(wedge_after, "phi", clockwise)
        wedge_high = lax.ppermute(wedge_before, "phi", counter)
        mass_across = lax.ppermute(mass, "phi", opposite)

        def sides(u, low, high, own, across, h, before, after, masses):
            for k in range(NV):
                for r in range(rows):
                    at = (k * rows + r) * 4
                    h[k, r, 0:4] = high[at : at + 4]
                    h[k, r, 4:8] = low[at : at + 4]
                for r in range(4):
                    before[k, r * wedge : (r + 1) * wedge] = u[k, r]
                    after[k, r * wedge : (r + 1) * wedge] = u[k, rows - 4 + r]
                for r in range(2):
                    at = 4 * wedge + 8 * r
                    before[k, at : at + 8] = h[k, r]
                    after[k, at : at + 8] = h[k, rows - 2 + r]
            beside = low[side_rows : side_rows + 8] + high[side_rows : side_rows + 8]
            total = (own[...] + across[...]) + beside
            masses[...] = jnp.concatenate([total] * (radial_devices // 8), axis=0)

        edge = shape(NV, 4 * wedge + 16, LANES)
        h, before, after, masses = pl.pallas_call(
            sides,
            out_shape=[shape(NV, rows, 8, LANES), edge, edge, shape(radial_devices, LANES)],
            in_specs=[vmem] * 5,
            out_specs=[vmem] * 4,
            compiler_params=limit,
            name="sides",
        )(conserved, wedge_low, wedge_high, mass, mass_across)

        low = lax.ppermute(after, "radial", up)
        high = lax.ppermute(before, "radial", down)
        everyone = lax.all_to_all(masses, "radial", 0, 0, tiled=True)

        def first_section(where, u, h, low, high, angles, out, pulled, x, radial_flux, left_row):
            ones = jnp.ones((8, LANES), f32)
            for k in range(NV):
                for r in range(4):
                    x[k, r, 0:wedge] = low[k, r * wedge : (r + 1) * wedge]
                    x[k, rows + 4 + r, 0:wedge] = high[k, r * wedge : (r + 1) * wedge]
                for r in range(2):
                    at = 4 * wedge + 8 * r
                    x[k, r, wedge:ring] = ones
                    x[k, r + 2, wedge:ring] = low[k, at : at + 8]
                    x[k, rows + 4 + r, wedge:ring] = high[k, at : at + 8]
                    x[k, rows + 6 + r, wedge:ring] = ones
                for r in range(rows):
                    x[k, r + 4, 0:wedge] = u[k, r]
                    x[k, r + 4, wedge:ring] = h[k, r]
            fill_ends(x, rows, where[0], radial_devices - 1)

            def emit(r, state, rate):
                for k in range(NV):
                    out[k, r] = state[k] + timestep * rate[k]
                pulled[0, r] = jnp.maximum(state[0], MINIMUM_DENSITY)
                pulled[1, r] = state[1]

            rate_rows(x, radial_flux, left_row, angles, outer, ring, where[0] * rows - 2, steps, emit)

        partial, pulled = pl.pallas_call(
            first_section,
            out_shape=[shape(NV, outer, ring, LANES), shape(2, outer, ring, LANES)],
            in_specs=[smem] + [vmem] * 5,
            out_specs=[vmem] * 2,
            scratch_shapes=[
                pltpu.VMEM((NV, rows + 8, ring, LANES), f32),
                pltpu.VMEM((outer + 1, NV, ring, LANES), f32),
                pltpu.VMEM((NV, ring, LANES), f32),
            ],
            compiler_params=limit,
            name="first_section",
        )(position, conserved, h, low, high, table)

        def second_section(where, core, masses, u, part, pulled, angles, out, enclosed, x, radial_flux, left_row, pulls):
            first = where[0] * rows
            device = lax.broadcasted_iota(jnp.int32, (radial_devices, LANES), 0)
            lane = lax.broadcasted_iota(jnp.int32, (radial_devices, LANES), 1)
            zone = device * rows + lane
            shell = jnp.where(lane < rows, masses[...], 0.0)
            line = jnp.zeros((1, LANES), f32)
            for j in range(outer):
                index = first + (j - 2)
                weight = jnp.where(zone < index, 1.0, jnp.where(zone == index, 0.5, 0.0))
                inside = jnp.sum(shell * weight, axis=(0, 1), keepdims=True) + core[0]
                radius = radius_at(index.astype(f32))
                pull = (timestep * strength) * inside / (radius * radius)
                pulls[j] = pull
                line = jnp.where(lane[0:1] == j - 2, inside, line)
                for k in range(NV):
                    if k == 1:
                        x[k, j] = part[k, j] - pull * pulled[0, j]
                    elif k == 4:
                        x[k, j] = part[k, j] - pull * pulled[1, j]
                    else:
                        x[k, j] = part[k, j]
            enclosed[...] = line
            fill_ends(x, rows, where[0], radial_devices - 1)

            def emit(r, state, rate):
                pull = pulls[r + 2]
                density = jnp.maximum(state[0], MINIMUM_DENSITY)
                for k in range(NV):
                    change = timestep * rate[k]
                    if k == 1:
                        change = change - pull * density
                    if k == 4:
                        change = change - pull * state[1]
                    out[k, r] = 0.5 * u[k, r] + 0.5 * (state[k] + change)

            rate_rows(x, radial_flux, left_row, angles, rows, wedge, first, steps, emit)

        advanced, enclosed = pl.pallas_call(
            second_section,
            out_shape=[shape(*conserved.shape), shape(1, LANES)],
            in_specs=[smem, smem] + [vmem] * 5,
            out_specs=[vmem] * 2,
            scratch_shapes=[
                pltpu.VMEM((NV, outer, ring, LANES), f32),
                pltpu.VMEM((rows + 1, NV, wedge, LANES), f32),
                pltpu.VMEM((NV, wedge, LANES), f32),
                pltpu.VMEM((outer, 1, LANES), f32),
            ],
            compiler_params=limit,
            name="second_section",
        )(position, core_mass, everyone, conserved, partial, pulled, table)
        return advanced, enclosed[0, :rows]

    in_specs = (P(None, "radial", "phi", None), P())
    out_specs = (P(None, "radial", "phi", None), P("radial"))
    return jax.shard_map(body, mesh=mesh, in_specs=in_specs, out_specs=out_specs, check_vma=False)
```

time: 79.7 us -> 43.2 us (0.54)
  the two profiles are of different devices: /device:TPU:2 before, /device:TPU:1 now
where the time goes in v1:
time: 43.2 us; the launch traced here: 42.9 us
  starting transfers between devices  21.9 us (51%)
  Pallas kernels  11.4 us (26%)
  waiting for transfers between devices  4.94 us (11%)
  local copies, waits for them, and re-layouts  3.29 us (8%)
  between operations  1.36 us (3%)
    all_to_all x1, starting transfers between devices, body(): everyone = lax.all_to_all(masses, 'radial', 0, 0, tiled=True)  12.7 us
    pallas_call x1, Pallas kernels, body(): pl.pallas_call(first_section, out_shape=[shape(NV, outer, ring, LANES), s...  6.07 us
    pallas_call x1, Pallas kernels, body(): pl.pallas_call(second_section, out_shape=[shape(*conserved.shape), shape(...  4.55 us
    ppermute x1, starting transfers between devices, body(): low = lax.ppermute(after, 'radial', up)  3.72 us
    unnamed x10, local copies, waits for them, and re-layouts  2.77 us
    all_to_all x1, waiting for transfers between devices, body(): everyone = lax.all_to_all(masses, 'radial', 0, 0, tiled=True)  2.48 us
    ppermute x1, waiting for transfers between devices, body(): mass_across = lax.ppermute(mass, 'phi', opposite)  2.45 us
    ppermute x1, starting transfers between devices, body(): wedge_low = lax.ppermute(wedge_after, 'phi', clockwise)  2.19 us
  transfers between devices with their start and end apart: 6, of which 2 were waited for; matrix products, arithmetic and copies ran while one was open for 0% of the time, Pallas kernels for 14%

profile of v1, /device:TPU:1, one launch (start us, length us, event | category | flops | bytes accessed | tf_op | source)
XLA Modules:
  0.0 42.9 jit_solution(5528909302753161134)
XLA Ops:
  0.6 0.0 copy-start.4
  0.6 0.0 copy-start
  0.7 1.0 %copy-done = f32[8,8,16,128]{3,2,1,0:T(8,128)S(1)} copy-done((f32[8,8,16,128]{3,2,1,0:T(8,128)S(1)}, f32[8,8,16,128]{3,2,1,0:T(8,128)}, u32[]{:S(2)}) %copy-start) | copy-done | bytes 524312
  1.7 0.0 copy-start.3
  1.7 0.7 %copy-done.3 = f32[8,128]{1,0:T(8,128)S(1)} copy-done((f32[8,128]{1,0:T(8,128)S(1)}, f32[8,128]{1,0:T(8,128)}, u32[]{:S(2)}) %copy-start.3) | copy-done | bytes 4120
  2.4 0.0 copy-start.2
  2.4 0.1 pack.1
  2.5 2.2 %collective-permute-start = (f32[264,128]{1,0:T(8,128)S(1)}, f32[264,128]{1,0:T(8,128)S(1)}, u32[]{:S(2)}, u32[]{:S(2)}) collective-permute-start(f32[264,128]{1,0:T(8,128)S(1)} %get-tuple-element.13), channel_id=1, source_target_pairs={{0,1},{1,2},{2,3},{3,0},{4,5},{5,6},{6,7},{7,4},{8,9},{9,10},{10,1... | collective-permute-start | bytes 405512 | tf_op jit(solution)/shard_map/ppermute | solution.py:230
  4.7 1.5 %collective-permute-start.1 = (f32[264,128]{1,0:T(8,128)S(1)}, f32[264,128]{1,0:T(8,128)S(1)}, u32[]{:S(2)}, u32[]{:S(2)}) collective-permute-start(f32[264,128]{1,0:T(8,128)S(1)} %get-tuple-element.14), channel_id=1, source_target_pairs={{1,0},{2,1},{3,2},{0,3},{5,4},{6,5},{7,6},{4,7},{9,8},{10,9},{11,1... | collective-permute-start | bytes 405512 | tf_op jit(solution)/shard_map/ppermute | solution.py:231
  6.2 1.6 %collective-permute-start.2 = (f32[8,128]{1,0:T(8,128)S(1)}, f32[8,128]{1,0:T(8,128)S(1)}, u32[]{:S(2)}, u32[]{:S(2)}) collective-permute-start(f32[8,128]{1,0:T(8,128)S(1)} %get-tuple-element.15.own), channel_id=1, source_target_pairs={{0,2},{1,3},{2,0},{3,1},{4,6},{5,7},{6,4},{7,5},{8,10},{9,11},{10,... | collective-permute-start | bytes 12296 | tf_op jit(solution)/shard_map/ppermute | solution.py:232
  7.8 2.4 %collective-permute-done.2.across = f32[8,128]{1,0:T(8,128)S(1)} collective-permute-done((f32[8,128]{1,0:T(8,128)S(1)}, f32[8,128]{1,0:T(8,128)S(1)}, u32[]{:S(2)}, u32[]{:S(2)}) %collective-permute-start.2) | collective-permute-done | bytes 4128 | tf_op jit(solution)/shard_map/ppermute | solution.py:232
  10.2 0.0 collective-permute-done.low
  10.2 0.0 collective-permute-done.1.high
  10.2 0.0 copy-start.1
  10.3 1.0 %copy-done.1 = f32[8,8,16,128]{3,2,1,0:T(8,128)S(1)} copy-done((f32[8,8,16,128]{3,2,1,0:T(8,128)S(1)}, f32[8,8,16,128]{3,2,1,0:T(8,128)}, u32[]{:S(2)}) %copy-start.1) | copy-done | bytes 524312
  11.3 0.7 %sides.1 = (f32[8,8,8,128]{3,2,1,0:T(8,128)S(1)}, f32[8,80,128]{2,1,0:T(8,128)S(1)}, f32[8,80,128]{2,1,0:T(8,128)S(1)}, f32[64,128]{1,0:T(8,128)}) custom-call(f32[8,8,16,128]{3,2,1,0:T(8,128)S(1)} %copy-done.1, f32[264,128]{1,0:T(8,128)S(1)} %collective-permute-done.low, f32[264,128]{1,0:T(8,128)S(1)} %collective-permute-done.1.high, ...), custom_call_target="tpu_custom_call" | custom-call | tf_op jit(solution)/shard_map/sides/pallas_call | solution.py:252
  12.0 3.7 %collective-permute-start.3 = (f32[8,80,128]{2,1,0:T(8,128)S(1)}, f32[8,80,128]{2,1,0:T(8,128)S(1)}, u32[]{:S(2)}, u32[]{:S(2)}) collective-permute-start(f32[8,80,128]{2,1,0:T(8,128)S(1)} %get-tuple-element.18), channel_id=1, source_target_pairs={{0,4},{4,8},{8,12},{12,16},{16,20},{20,24},{24,28},{28,32},{32,36}... | collective-permute-start | bytes 983048 | tf_op jit(solution)/shard_map/ppermute | solution.py:261
  15.7 0.2 collective-permute-start.4
  15.9 12.7 %all-to-all-start = ((f32[64,1,128]{2,1,0:T(1,128)}), f32[64,1,128]{2,1,0:T(1,128)S(1)}, u32[]{:S(2)}, u32[]{:S(2)}) async-start(f32[64,1,128]{2,1,0:T(1,128)} %bitcast.2), calls=%async_computation | async-start | bytes 65536 | tf_op jit(solution)/shard_map/all_to_all | solution.py:263
  29.3 0.0 collective-permute-done.3.low
  29.3 0.0 collective-permute-done.4.high
  29.3 0.0 copy-done.4
  29.3 0.0 copy-done.2
  29.3 6.1 %first_section.1 = (f32[8,12,24,128]{3,2,1,0:T(8,128)S(1)}, f32[2,12,24,128]{3,2,1,0:T(8,128)S(1)}) custom-call(s32[1]{0:T(128)} %bitcast.where, f32[8,8,16,128]{3,2,1,0:T(8,128)S(1)} %copy-done.2, f32[8,8,8,128]{3,2,1,0:T(8,128)S(1)} %get-tuple-element.17.h, f32[8,80,128]{2,1,0:T(8,128)S(1)} %collective-permute-done.3.low, ...), custom_call_target="tpu_custom_call" | custom-call | tf_op jit(solution)/shard_map/first_section/pallas_call | solution.py:290
  35.4 2.5 %all-to-all-done = f32[64,1,128]{2,1,0:T(1,128)S(1)} async-done(((f32[64,1,128]{2,1,0:T(1,128)}), f32[64,1,128]{2,1,0:T(1,128)S(1)}, u32[]{:S(2)}, u32[]{:S(2)}) %all-to-all-start) | async-done | bytes 32800 | tf_op jit(solution)/shard_map/all_to_all | solution.py:263
  37.9 4.5 %second_section.1 = (f32[8,8,16,128]{3,2,1,0:T(8,128)}, f32[1,128]{1,0:T(1,128)S(1)}) custom-call(s32[1]{0:T(128)} %bitcast.where, f32[1]{0:T(128)S(6)} %copy.6.core, f32[64,128]{1,0:T(8,128)S(1)} %bitcast.7, f32[8,8,16,128]{3,2,1,0:T(8,128)S(1)} %copy-done.2, f32[8,12,24,128]{3,2,1,0:T(8,128)S(1)} %get-tuple-element.20.part, ...), custom_call_target="tpu_custom_call" | custom-call | tf_op jit(solution)/shard_map/second_section/pallas_call | solution.py:342
  42.4 0.5 %slice_bitcast_fusion = f32[8]{0:T(128)} fusion(f32[1,128]{1,0:T(1,128)S(1)} %get-tuple-element.23), kind=kLoop, calls=%fused_computation | loop fusion | bytes 64 | tf_op jit(solution)/shard_map/squeeze | solution.py:356
Async XLA Ops:
  0.6 28.7 %copy-start.4 = (f32[8,128]{1,0:T(8,128)S(1)}, f32[8,128]{1,0:T(8,128)}, u32[]{:S(2)}) copy-start(f32[8,128]{1,0:T(8,128)} %constant.8.clone.angles) | copy-start | bytes 12292
  0.6 1.0 %copy-start = (f32[8,8,16,128]{3,2,1,0:T(8,128)S(1)}, f32[8,8,16,128]{3,2,1,0:T(8,128)}, u32[]{:S(2)}) copy-start(f32[8,8,16,128]{3,2,1,0:T(8,128)} %u.7) | copy-start | bytes 1572868
  1.7 0.7 %copy-start.3 = (f32[8,128]{1,0:T(8,128)S(1)}, f32[8,128]{1,0:T(8,128)}, u32[]{:S(2)}) copy-start(f32[8,128]{1,0:T(8,128)} %constant.8.clone.angles) | copy-start | bytes 12292
  2.4 26.9 %copy-start.2 = (f32[8,8,16,128]{3,2,1,0:T(8,128)S(1)}, f32[8,8,16,128]{3,2,1,0:T(8,128)}, u32[]{:S(2)}) copy-start(f32[8,8,16,128]{3,2,1,0:T(8,128)} %u.7) | copy-start | bytes 1572868
  2.5 7.7 %collective-permute-start = (f32[264,128]{1,0:T(8,128)S(1)}, f32[264,128]{1,0:T(8,128)S(1)}, u32[]{:S(2)}, u32[]{:S(2)}) collective-permute-start(f32[264,128]{1,0:T(8,128)S(1)} %get-tuple-element.13), channel_id=1, source_target_pairs={{0,1},{1,2},{2,3},{3,0},{4,5},{5,6},{6,7},{7,4},{8,9},{9,10},{10,1... | collective-permute-start | bytes 405512 | tf_op jit(solution)/shard_map/ppermute | solution.py:230
  4.7 5.5 %collective-permute-start.1 = (f32[264,128]{1,0:T(8,128)S(1)}, f32[264,128]{1,0:T(8,128)S(1)}, u32[]{:S(2)}, u32[]{:S(2)}) collective-permute-start(f32[264,128]{1,0:T(8,128)S(1)} %get-tuple-element.14), channel_id=1, source_target_pairs={{1,0},{2,1},{3,2},{0,3},{5,4},{6,5},{7,6},{4,7},{9,8},{10,9},{11,1... | collective-permute-start | bytes 405512 | tf_op jit(solution)/shard_map/ppermute | solution.py:231
  6.2 4.0 %collective-permute-start.2 = (f32[8,128]{1,0:T(8,128)S(1)}, f32[8,128]{1,0:T(8,128)S(1)}, u32[]{:S(2)}, u32[]{:S(2)}) collective-permute-start(f32[8,128]{1,0:T(8,128)S(1)} %get-tuple-element.15.own), channel_id=1, source_target_pairs={{0,2},{1,3},{2,0},{3,1},{4,6},{5,7},{6,4},{7,5},{8,10},{9,11},{10,... | collective-permute-start | bytes 12296 | tf_op jit(solution)/shard_map/ppermute | solution.py:232
  10.2 1.0 %copy-start.1 = (f32[8,8,16,128]{3,2,1,0:T(8,128)S(1)}, f32[8,8,16,128]{3,2,1,0:T(8,128)}, u32[]{:S(2)}) copy-start(f32[8,8,16,128]{3,2,1,0:T(8,128)} %u.7) | copy-start | bytes 1572868
  12.0 17.3 %collective-permute-start.3 = (f32[8,80,128]{2,1,0:T(8,128)S(1)}, f32[8,80,128]{2,1,0:T(8,128)S(1)}, u32[]{:S(2)}, u32[]{:S(2)}) collective-permute-start(f32[8,80,128]{2,1,0:T(8,128)S(1)} %get-tuple-element.18), channel_id=1, source_target_pairs={{0,4},{4,8},{8,12},{12,16},{16,20},{20,24},{24,28},{28,32},{32,36}... | collective-permute-start | bytes 983048 | tf_op jit(solution)/shard_map/ppermute | solution.py:261
  15.7 13.6 %collective-permute-start.4 = (f32[8,80,128]{2,1,0:T(8,128)S(1)}, f32[8,80,128]{2,1,0:T(8,128)S(1)}, u32[]{:S(2)}, u32[]{:S(2)}) collective-permute-start(f32[8,80,128]{2,1,0:T(8,128)S(1)} %get-tuple-element.19), channel_id=1, source_target_pairs={{4,0},{8,4},{12,8},{16,12},{20,16},{24,20},{28,24},{32,28},{36,32}... | collective-permute-start | bytes 983048 | tf_op jit(solution)/shard_map/ppermute | solution.py:262
  15.9 22.0 %all-to-all-start = ((f32[64,1,128]{2,1,0:T(1,128)}), f32[64,1,128]{2,1,0:T(1,128)S(1)}, u32[]{:S(2)}, u32[]{:S(2)}) async-start(f32[64,1,128]{2,1,0:T(1,128)} %bitcast.2), calls=%async_computation | async-start | bytes 65536 | tf_op jit(solution)/shard_map/all_to_all | solution.py:263

commit v2 on v1

v2 whole, which is shorter than its diff:
```python
import math

import jax
import jax.numpy as jnp
from jax import lax
from jax.experimental import pallas as pl
from jax.experimental.pallas import tpu as pltpu
from jax.sharding import PartitionSpec as P

ADIABATIC = 4.0 / 3.0
INNER_RADIUS = 1.0
OUTER_RADIUS = 2.0
COURANT = 0.4
GRAVITY_KICK = 0.004
MINIMUM_DENSITY = 0.05
PRESSURE_FLOOR = 0.01
NV = 8
LANES = 128
SUBLANES = 8
UNROLL1 = 2
UNROLL2 = 4
VMEM_LIMIT = 12 * 1024 * 1024


def step_sizes(radial_total, phi_total, theta_total):
    theta_step = math.pi / theta_total
    phi_step = 2.0 * math.pi / phi_total
    polar_width = INNER_RADIUS * math.sin(0.5 * theta_step) * phi_step
    radial_step = min(2.0 * polar_width, (OUTER_RADIUS - INNER_RADIUS) / radial_total)
    timestep = COURANT * min(radial_step, polar_width)
    return (radial_step, theta_step, phi_step, timestep)


def splat(value):
    return jnp.full((SUBLANES, LANES), value, jnp.float32)


def lane_index():
    return lax.broadcasted_iota(jnp.int32, (SUBLANES, LANES), 1)


def sine_of_zones(theta_step):
    return jnp.sin((lane_index().astype(jnp.float32) + 0.5) * theta_step)


def fill_angles(angles, steps):
    _, theta_step, phi_step, _ = steps
    lane = lane_index().astype(jnp.float32)
    sine = sine_of_zones(theta_step)
    angles[0] = jnp.cos((lane + 0.5) * theta_step) / sine
    angles[1] = jnp.sin((lane + 1.0) * theta_step) * (0.5 / (sine * theta_step))
    angles[2] = jnp.sin(lane * theta_step) * (0.5 / (sine * theta_step))
    angles[3] = 0.5 / (sine * phi_step)


def half_slope(below, above):
    return 0.5 * jnp.maximum(jnp.minimum(above, jnp.maximum(below, 0.0)), jnp.minimum(below, 0.0))


def thermo(u):
    density = jnp.maximum(u[0], MINIMUM_DENSITY)
    inverse = 1.0 / density
    kinetic = (0.5 * inverse) * (u[1] * u[1] + u[2] * u[2] + u[3] * u[3])
    pressure = jnp.maximum((ADIABATIC - 1.0) * (u[4] - kinetic), PRESSURE_FLOOR * density)
    return density, inverse, pressure


def side(u, component):
    _, inverse, pressure = thermo(u)
    normal = u[component] * inverse
    square = (ADIABATIC * pressure) * inverse
    return normal, pressure, jnp.abs(normal) + square * lax.rsqrt(square)


def face_flux(left, right, component):
    vl, pl_, al = side(left, component)
    vr, pr, ar = side(right, component)
    signal = jnp.maximum(al, ar)
    toward, away = vl + signal, vr - signal
    out = [left[k] * toward + right[k] * away for k in range(NV)]
    out[component] = out[component] + (pl_ + pr)
    out[4] = out[4] + (pl_ * vl + pr * vr)
    return out


def next_zone(value, edge):
    turned = pltpu.roll(value, SUBLANES - 1, 1)
    return jnp.where(edge, jnp.concatenate([turned[1:], turned[:1]], axis=0), turned)


def previous_zone(value, edge):
    turned = pltpu.roll(value, 1, 1)
    return jnp.where(edge, jnp.concatenate([turned[-1:], turned[:-1]], axis=0), turned)


def rate_rows(x, kept, angles, rows, wide, first_row, steps, unroll, emit):
    radial_step = steps[0]

    def radius_of(index):
        return INNER_RADIUS + (splat(index) + 0.5) * radial_step

    def states(j, below):
        left, right, above = [], [], []
        for k in range(NV):
            centre = x[j, k, :wide]
            difference = x[j + 1, k, :wide] - centre
            slope = half_slope(below[k], difference)
            left.append(centre + slope)
            right.append(centre - slope)
            above.append(difference)
        return left, right, above

    def keep(left, above):
        for k in range(NV):
            kept[0, k] = left[k]
            kept[1, k] = above[k]

    def radial_face(f):
        inner = [kept[0, k] for k in range(NV)]
        left, right, above = states(f + 2, [kept[1, k] for k in range(NV)])
        keep(left, above)
        face = radius_of(jnp.asarray(first_row + f).astype(jnp.float32)) - 0.5 * radial_step
        area = (0.5 / radial_step) * face * face
        return [area * value for value in face_flux(inner, right, 1)]

    left, _, above = states(1, [x[1, k, :wide] - x[0, k, :wide] for k in range(NV)])
    keep(left, above)
    for k, value in enumerate(radial_face(0)):
        kept[2, k] = value

    last = lane_index() == LANES - 1
    sublane = lax.broadcasted_iota(jnp.int32, (SUBLANES, LANES), 0)
    top, bottom = sublane == SUBLANES - 1, sublane == 0

    def row(r, carry):
        inverse_radius = 1.0 / radius_of((first_row + r).astype(jnp.float32))
        radial_scale = inverse_radius * inverse_radius
        u = [x[r + 2, k, :wide] for k in range(NV)]
        upper = radial_face(r + 1)
        rate = [(kept[2, k] - upper[k]) * radial_scale for k in range(NV)]
        for k in range(NV):
            kept[2, k] = upper[k]
        left, right = [], []
        for k in range(NV):
            after = jnp.where(last, u[k], pltpu.roll(u[k], LANES - 1, 2))
            above = after - u[k]
            slope = half_slope(pltpu.roll(above, 1, 2), above)
            left.append(u[k] + slope)
            right.append(after - pltpu.roll(slope, LANES - 1, 2))
        flux = face_flux(left, right, 2)
        upper, lower = angles[1] * inverse_radius, angles[2] * inverse_radius
        for k in range(NV):
            rate[k] = rate[k] - (upper * flux[k] - lower * pltpu.roll(flux[k], 1, 2))
        left, right = [], []
        for k in range(NV):
            zones = x[r + 2, k]
            after = next_zone(zones, top)
            above = after - zones
            slope = half_slope(previous_zone(above, bottom), above)
            left.append(zones + slope)
            right.append(after - next_zone(slope, top))
        flux = face_flux(left, right, 3)
        scale = angles[3] * inverse_radius
        for k in range(NV):
            rate[k] = rate[k] - scale * (flux[k][:wide] - previous_zone(flux[k], bottom)[:wide])
        density, inverse, pressure = thermo(u)
        cotangent = angles[0]
        vr, vt, vp = u[1] * inverse, u[2] * inverse, u[3] * inverse
        azimuth_push = density * vp * vp
        polar_carry = density * vt
        rate[1] = rate[1] + (2.0 * pressure + (polar_carry * vt + azimuth_push)) * inverse_radius
        rate[2] = rate[2] + ((pressure + azimuth_push) * cotangent - polar_carry * vr) * inverse_radius
        rate[3] = rate[3] - density * vp * (vr + vt * cotangent) * inverse_radius
        emit(r, u, rate)
        return carry

    lax.fori_loop(0, rows, row, 0, unroll=unroll)


def fill_ends(x, rows, position, last_position):
    first = (x.shape[0] - rows) // 2
    last = first + rows - 1

    @pl.when(position == 0)
    def _():
        for k in range(NV):
            x[first - 2, k] = x[first, k]
            x[first - 1, k] = x[first, k]

    @pl.when(position == last_position)
    def _():
        for k in range(NV):
            x[last + 1, k] = x[last, k]
            x[last + 2, k] = x[last, k]


def solution(mesh):
    radial_devices, phi_devices = mesh.shape["radial"], mesh.shape["phi"]
    assert phi_devices == 4
    up = [(i, (i + 1) % radial_devices) for i in range(radial_devices)]
    down = [(j, i) for i, j in up]
    clockwise = [(i, (i + 1) % phi_devices) for i in range(phi_devices)]
    counter = [(j, i) for i, j in clockwise]
    opposite = [(i, (i + 2) % phi_devices) for i in range(phi_devices)]

    def body(conserved, core_mass):
        _, rows, wedge, theta_cells = conserved.shape
        steps = step_sizes(rows * radial_devices, wedge * phi_devices, theta_cells)
        radial_step, theta_step, phi_step, timestep = steps
        strength = GRAVITY_KICK / timestep
        own = wedge // SUBLANES
        tiles, outer = own + 1, rows + 4
        zones = conserved.reshape(NV, rows, own, SUBLANES, theta_cells)
        position = lax.axis_index("radial").astype(jnp.int32).reshape(1)
        smem = pl.BlockSpec(memory_space=pltpu.SMEM)
        vmem = pl.BlockSpec(memory_space=pltpu.VMEM)
        hbm = pl.BlockSpec(memory_space=pl.ANY)
        f32 = jnp.float32
        limit = pltpu.CompilerParams(vmem_limit_bytes=VMEM_LIMIT)
        angle_scratch = pltpu.VMEM((4, SUBLANES, LANES), f32)

        def shape(*sizes):
            return jax.ShapeDtypeStruct(sizes, f32)

        def radius_at(index):
            return INNER_RADIUS + (splat(index) + 0.5) * radial_step

        def whole(value):
            return jnp.sum(value, axis=(0, 1), keepdims=True)

        side_rows = NV * rows * 4
        corner = 4 * own

        def pack(where, u, mass, wedge_before, wedge_after, before, after):
            sine = sine_of_zones(theta_step)
            lane = lane_index()
            tile = jnp.zeros((SUBLANES, LANES), f32)
            for r in range(rows):
                radius = radius_at((where[0] * rows + r).astype(f32))
                total = sum(u[0, r, t] for t in range(1, own)) + u[0, r, 0]
                shell = whole(total * sine) * (radius * radius * (radial_step * theta_step * phi_step))
                tile = jnp.where(lane == r, shell, tile)
            mass[...] = tile
            wedge_before[side_rows : side_rows + 8] = tile
            wedge_after[side_rows : side_rows + 8] = tile
            for k in range(NV):
                for r in range(rows):
                    at = (k * rows + r) * 4
                    wedge_before[at : at + 4] = u[k, r, 0, 0:4]
                    wedge_after[at : at + 4] = u[k, r, own - 1, 4:8]
                for r in range(4):
                    for t in range(own):
                        before[k, r * own + t] = u[k, r, t]
                        after[k, r * own + t] = u[k, rows - 4 + r, t]

        edge = shape(NV, corner + 2, SUBLANES, LANES)
        mass, wedge_before, wedge_after, before, after = pl.pallas_call(
            pack,
            out_shape=[shape(8, LANES), shape(side_rows + 8, LANES), shape(side_rows + 8, LANES), edge, edge],
            in_specs=[smem, vmem],
            out_specs=[vmem] * 5,
            compiler_params=limit,
            name="pack",
        )(position, zones)

        wedge_low = lax.ppermute(wedge_after, "phi", clockwise)
        wedge_high = lax.ppermute(wedge_before, "phi", counter)
        mass_across = lax.ppermute(mass, "phi", opposite)

        def sides(low, high, mass, across, _before, _after, h, before, after, masses):
            for k in range(NV):
                for r in range(rows):
                    at = (k * rows + r) * 4
                    h[k, r, 0:4] = high[at : at + 4]
                    h[k, r, 4:8] = low[at : at + 4]
                for r in range(2):
                    before[k, corner + r] = h[k, r]
                    after[k, corner + r] = h[k, rows - 2 + r]
            beside = low[side_rows : side_rows + 8] + high[side_rows : side_rows + 8]
            total = (mass[...] + across[...]) + beside
            masses[...] = jnp.concatenate([total] * (radial_devices // 8), axis=0)

        h, before, after, masses = pl.pallas_call(
            sides,
            out_shape=[shape(NV, rows, SUBLANES, LANES), edge, edge, shape(radial_devices, LANES)],
            in_specs=[vmem] * 6,
            out_specs=[vmem] * 4,
            input_output_aliases={4: 1, 5: 2},
            compiler_params=limit,
            name="sides",
        )(wedge_low, wedge_high, mass, mass_across, before, after)

        low = lax.ppermute(after, "radial", up)
        high = lax.ppermute(before, "radial", down)
        everyone = lax.all_to_all(masses, "radial", 0, 0, tiled=True)

        def first_section(where, u, h, low, high, out, pulled, x, kept, angles):
            fill_angles(angles, steps)
            ones = splat(1.0)
            for k in range(NV):
                for r in range(4):
                    for t in range(own):
                        x[r, k, t] = low[k, r * own + t]
                        x[rows + 4 + r, k, t] = high[k, r * own + t]
                for r in range(2):
                    x[r, k, own] = ones
                    x[r + 2, k, own] = low[k, corner + r]
                    x[rows + 4 + r, k, own] = high[k, corner + r]
                    x[rows + 6 + r, k, own] = ones
                for r in range(rows):
                    for t in range(own):
                        x[r + 4, k, t] = u[k, r, t]
                    x[r + 4, k, own] = h[k, r]
            fill_ends(x, rows, where[0], radial_devices - 1)

            def emit(r, state, rate):
                for k in range(NV):
                    out[r, k] = state[k] + timestep * rate[k]
                pulled[r, 0] = jnp.maximum(state[0], MINIMUM_DENSITY)
                pulled[r, 1] = state[1]

            rate_rows(x, kept, angles, outer, tiles, where[0] * rows - 2, steps, UNROLL1, emit)

        partial, pulled = pl.pallas_call(
            first_section,
            out_shape=[shape(outer, NV, tiles, SUBLANES, LANES), shape(outer, 2, tiles, SUBLANES, LANES)],
            in_specs=[smem] + [vmem] * 4,
            out_specs=[vmem] * 2,
            scratch_shapes=[
                pltpu.VMEM((rows + 8, NV, tiles, SUBLANES, LANES), f32),
                pltpu.VMEM((3, NV, tiles, SUBLANES, LANES), f32),
                angle_scratch,
            ],
            compiler_params=limit,
            name="first_section",
        )(position, zones, h, low, high)

        def second_section(
            where, core, masses, u, part, pulled, out, enclosed,
            x, kept, angles, pulls, done, sent,
        ):
            fill_angles(angles, steps)
            first = where[0] * rows
            device = lax.broadcasted_iota(jnp.int32, (radial_devices, LANES), 0)
            lane = lax.broadcasted_iota(jnp.int32, (radial_devices, LANES), 1)
            zone = device * rows + lane
            shell = jnp.where(lane < rows, masses[...], 0.0)
            line = jnp.zeros((1, LANES), f32)
            for j in range(outer):
                index = first + (j - 2)
                weight = jnp.where(zone < index, 1.0, jnp.where(zone == index, 0.5, 0.0))
                inside = whole(shell * weight) + core[0]
                radius = radius_at(index.astype(f32))
                pull = (timestep * strength) * inside / (radius * radius)
                pulls[j] = pull
                line = jnp.where(lane[0:1] == j - 2, inside, line)
                for k in range(NV):
                    if k == 1:
                        x[j, k] = part[j, k] - pull * pulled[j, 0]
                    elif k == 4:
                        x[j, k] = part[j, k] - pull * pulled[j, 1]
                    else:
                        x[j, k] = part[j, k]
            enclosed[...] = line[:, :rows]
            fill_ends(x, rows, where[0], radial_devices - 1)

            def leave(r):
                return pltpu.make_async_copy(done.at[r], out.at[:, r], sent.at[r])

            def emit(r, state, rate):
                pull = pulls[r + 2]
                density = jnp.maximum(state[0], MINIMUM_DENSITY)
                for k in range(NV):
                    change = timestep * rate[k]
                    if k == 1:
                        change = change - pull * density
                    if k == 4:
                        change = change - pull * state[1]
                    done[r, k] = 0.5 * u[k, r] + 0.5 * (state[k] + change)
                leave(r).start()

            rate_rows(x, kept, angles, rows, own, first, steps, UNROLL2, emit)
            for r in range(rows):
                leave(r).wait()

        advanced, enclosed = pl.pallas_call(
            second_section,
            out_shape=[shape(*zones.shape), shape(1, rows)],
            in_specs=[smem, smem] + [vmem] * 4,
            out_specs=[hbm, vmem],
            scratch_shapes=[
                pltpu.VMEM((outer, NV, tiles, SUBLANES, LANES), f32),
                pltpu.VMEM((3, NV, own, SUBLANES, LANES), f32),
                angle_scratch,
                pltpu.VMEM((outer, SUBLANES, LANES), f32),
                pltpu.VMEM((rows, NV, own, SUBLANES, LANES), f32),
                pltpu.SemaphoreType.DMA((rows,)),
            ],
            compiler_params=limit,
            name="second_section",
        )(position, core_mass, everyone, zones, partial, pulled)
        return advanced.reshape(conserved.shape), enclosed.reshape(rows)

    in_specs = (P(None, "radial", "phi", None), P())
    out_specs = (P(None, "radial", "phi", None), P("radial"))
    return jax.shard_map(body, mesh=mesh, in_specs=in_specs, out_specs=out_specs, check_vma=False)
```

time: 43.2 us -> 39.8 us (0.921)
  Pallas kernels: 11.4 us -> 8.52 us
  local copies, waits for them, and re-layouts: 3.29 us -> 1.04 us
  waiting for transfers between devices: 4.94 us -> 6.82 us
    pallas_call x3, Pallas kernels: 11.3 us -> 8.35 us  [the longest x1 4.19 us: body(): pl.pallas_call(first_section, out_shape=[shape(outer, NV, tiles, SUBLANES...]
    all_to_all x1, waiting for transfers between devices: 2.48 us -> 4.36 us  [body(): everyone = lax.all_to_all(masses, 'radial', 0, 0, tiled=True)]
    unnamed x10 -> x4, local copies, waits for them, and re-layouts: 2.77 us -> 1.04 us
    squeeze x1 -> x0, local copies, waits for them, and re-layouts: 0.51 us -> none  [body(): return (advanced, enclosed[0, :rows])]
  transfers between devices with their start and end apart: 6 -> 6, of which waited for: 2 -> 2; matrix products, arithmetic and copies ran while one was open for 0% -> 0% of each run, Pallas kernels for 14% -> 11%
where the time goes in v2:
time: 39.8 us; the launch traced here: 39.6 us
  starting transfers between devices  21.9 us (55%)
  Pallas kernels  8.52 us (21%)
  waiting for transfers between devices  6.82 us (17%)
  between operations  1.34 us (3%)
  local copies, waits for them, and re-layouts  1.04 us (3%)
    all_to_all x1, starting transfers between devices, body(): everyone = lax.all_to_all(masses, 'radial', 0, 0, tiled=True)  12.7 us
    all_to_all x1, waiting for transfers between devices, body(): everyone = lax.all_to_all(masses, 'radial', 0, 0, tiled=True)  4.36 us
    pallas_call x1, Pallas kernels, body(): pl.pallas_call(first_section, out_shape=[shape(outer, NV, tiles, SUBLANES...  4.19 us
    ppermute x1, starting transfers between devices, body(): low = lax.ppermute(after, 'radial', up)  3.72 us
    pallas_call x1, Pallas kernels, body(): pl.pallas_call(second_section, out_shape=[shape(*zones.shape), shape(1, r...  3.47 us
    ppermute x1, waiting for transfers between devices, body(): mass_across = lax.ppermute(mass, 'phi', opposite)  2.45 us
    ppermute x1, starting transfers between devices, body(): wedge_low = lax.ppermute(wedge_after, 'phi', clockwise)  2.19 us
    ppermute x1, starting transfers between devices, body(): mass_across = lax.ppermute(mass, 'phi', opposite)  1.56 us
  transfers between devices with their start and end apart: 6, of which 2 were waited for; matrix products, arithmetic and copies ran while one was open for 0% of the time, Pallas kernels for 11%

profile of v2, /device:TPU:1, one launch (start us, length us, event | category | flops | bytes accessed | tf_op | source)
XLA Modules:
  0.0 39.6 jit_solution(695412230839255245)
XLA Ops:
  0.6 0.0 copy-start
  0.6 1.0 %copy-done = f32[8,8,16,128]{3,2,1,0:T(8,128)S(1)} copy-done((f32[8,8,16,128]{3,2,1,0:T(8,128)S(1)}, f32[8,8,16,128]{3,2,1,0:T(8,128)}, u32[]{:S(2)}) %copy-start) | copy-done | bytes 524312
  1.7 0.0 copy-start.1
  1.7 0.2 pack.1
  1.9 2.2 %collective-permute-start = (f32[264,128]{1,0:T(8,128)S(1)}, f32[264,128]{1,0:T(8,128)S(1)}, u32[]{:S(2)}, u32[]{:S(2)}) collective-permute-start(f32[264,128]{1,0:T(8,128)S(1)} %get-tuple-element.15), channel_id=1, source_target_pairs={{0,1},{1,2},{2,3},{3,0},{4,5},{5,6},{6,7},{7,4},{8,9},{9,10},{10,1... | collective-permute-start | bytes 405512 | tf_op jit(solution)/shard_map/ppermute | solution.py:266
  4.1 1.5 %collective-permute-start.1 = (f32[264,128]{1,0:T(8,128)S(1)}, f32[264,128]{1,0:T(8,128)S(1)}, u32[]{:S(2)}, u32[]{:S(2)}) collective-permute-start(f32[264,128]{1,0:T(8,128)S(1)} %get-tuple-element.16), channel_id=1, source_target_pairs={{1,0},{2,1},{3,2},{0,3},{5,4},{6,5},{7,6},{4,7},{9,8},{10,9},{11,1... | collective-permute-start | bytes 405512 | tf_op jit(solution)/shard_map/ppermute | solution.py:267
  5.6 1.6 %collective-permute-start.2 = (f32[8,128]{1,0:T(8,128)S(1)}, f32[8,128]{1,0:T(8,128)S(1)}, u32[]{:S(2)}, u32[]{:S(2)}) collective-permute-start(f32[8,128]{1,0:T(8,128)S(1)} %get-tuple-element.17.mass), channel_id=1, source_target_pairs={{0,2},{1,3},{2,0},{3,1},{4,6},{5,7},{6,4},{7,5},{8,10},{9,11},{10,... | collective-permute-start | bytes 12296 | tf_op jit(solution)/shard_map/ppermute | solution.py:268
  7.1 2.4 %collective-permute-done.2.across = f32[8,128]{1,0:T(8,128)S(1)} collective-permute-done((f32[8,128]{1,0:T(8,128)S(1)}, f32[8,128]{1,0:T(8,128)S(1)}, u32[]{:S(2)}, u32[]{:S(2)}) %collective-permute-start.2) | collective-permute-done | bytes 4128 | tf_op jit(solution)/shard_map/ppermute | solution.py:268
  9.6 0.0 collective-permute-done.low
  9.6 0.0 collective-permute-done.1.high
  9.6 0.7 %sides.1 = (f32[8,8,8,128]{3,2,1,0:T(8,128)S(1)}, f32[8,10,8,128]{3,2,1,0:T(8,128)S(1)}, f32[8,10,8,128]{3,2,1,0:T(8,128)S(1)}, f32[64,128]{1,0:T(8,128)}) custom-call(f32[264,128]{1,0:T(8,128)S(1)} %collective-permute-done.low, f32[264,128]{1,0:T(8,128)S(1)} %collective-permute-done.1.high, ...), custom_call_target="tpu_custom_call", output_to_operand_aliasing={{1}: (4, {}), {2}: (5, {})} | custom-call | tf_op jit(solution)/shard_map/sides/pallas_call | solution.py:283
  10.3 3.7 %collective-permute-start.3 = (f32[8,10,8,128]{3,2,1,0:T(8,128)S(1)}, f32[8,10,8,128]{3,2,1,0:T(8,128)S(1)}, u32[]{:S(2)}, u32[]{:S(2)}) collective-permute-start(f32[8,10,8,128]{3,2,1,0:T(8,128)S(1)} %get-tuple-element.22), channel_id=1, source_target_pairs={{0,4},{4,8},{8,12},{12,16},{16,20},{20,24},{24,28},{28,32},{32,36}... | collective-permute-start | bytes 983048 | tf_op jit(solution)/shard_map/ppermute | solution.py:293
  14.0 0.2 collective-permute-start.4
  14.2 12.7 %all-to-all-start = ((f32[64,1,128]{2,1,0:T(1,128)}), f32[64,1,128]{2,1,0:T(1,128)S(1)}, u32[]{:S(2)}, u32[]{:S(2)}) async-start(f32[64,1,128]{2,1,0:T(1,128)} %bitcast.3), calls=%async_computation | async-start | bytes 65536 | tf_op jit(solution)/shard_map/all_to_all | solution.py:295
  27.6 0.0 collective-permute-done.3.low
  27.6 0.0 collective-permute-done.4.high
  27.6 0.0 copy-done.1
  27.6 4.2 %first_section.1 = (f32[12,8,3,8,128]{4,3,2,1,0:T(8,128)S(1)}, f32[12,2,3,8,128]{4,3,2,1,0:T(8,128)S(1)}) custom-call(s32[1]{0:T(128)} %bitcast.where, f32[8,8,2,8,128]{4,3,2,1,0:T(8,128)S(1)} %bitcast.9, f32[8,8,8,128]{3,2,1,0:T(8,128)S(1)} %get-tuple-element.21.h, f32[8,10,8,128]{3,2,1,0:T(8,128)S(1)} %collective-permute-done.3.low, ...), custom_call_target="tpu_custom_call" | custom-call | tf_op jit(solution)/shard_map/first_section/pallas_call | solution.py:324
  31.8 4.4 %all-to-all-done = f32[64,1,128]{2,1,0:T(1,128)S(1)} async-done(((f32[64,1,128]{2,1,0:T(1,128)}), f32[64,1,128]{2,1,0:T(1,128)S(1)}, u32[]{:S(2)}, u32[]{:S(2)}) %all-to-all-start) | async-done | bytes 32800 | tf_op jit(solution)/shard_map/all_to_all | solution.py:295
  36.2 3.5 %second_section.1 = (f32[8,8,2,8,128]{4,3,2,1,0:T(8,128)}, f32[1,8]{1,0:T(1,128)}) custom-call(s32[1]{0:T(128)} %bitcast.where, f32[1]{0:T(128)S(6)} %copy.9.core, f32[64,128]{1,0:T(8,128)S(1)} %bitcast.11, f32[8,8,2,8,128]{4,3,2,1,0:T(8,128)S(1)} %bitcast.10, f32[12,8,3,8,128]{4,3,2,1,0:T(8,128)S(1)} %get-tuple-element.24.part, ...), custom_call_target="tpu_custom_call" | custom-call | tf_op jit(solution)/shard_map/second_section/pallas_call | solution.py:386
Async XLA Ops:
  0.6 1.0 %copy-start = (f32[8,8,16,128]{3,2,1,0:T(8,128)S(1)}, f32[8,8,16,128]{3,2,1,0:T(8,128)}, u32[]{:S(2)}) copy-start(f32[8,8,16,128]{3,2,1,0:T(8,128)} %param.2) | copy-start | bytes 1572868
  1.7 25.9 %copy-start.1 = (f32[8,8,16,128]{3,2,1,0:T(8,128)S(1)}, f32[8,8,16,128]{3,2,1,0:T(8,128)}, u32[]{:S(2)}) copy-start(f32[8,8,16,128]{3,2,1,0:T(8,128)} %param.2) | copy-start | bytes 1572868
  1.9 7.7 %collective-permute-start = (f32[264,128]{1,0:T(8,128)S(1)}, f32[264,128]{1,0:T(8,128)S(1)}, u32[]{:S(2)}, u32[]{:S(2)}) collective-permute-start(f32[264,128]{1,0:T(8,128)S(1)} %get-tuple-element.15), channel_id=1, source_target_pairs={{0,1},{1,2},{2,3},{3,0},{4,5},{5,6},{6,7},{7,4},{8,9},{9,10},{10,1... | collective-permute-start | bytes 405512 | tf_op jit(solution)/shard_map/ppermute | solution.py:266
  4.1 5.5 %collective-permute-start.1 = (f32[264,128]{1,0:T(8,128)S(1)}, f32[264,128]{1,0:T(8,128)S(1)}, u32[]{:S(2)}, u32[]{:S(2)}) collective-permute-start(f32[264,128]{1,0:T(8,128)S(1)} %get-tuple-element.16), channel_id=1, source_target_pairs={{1,0},{2,1},{3,2},{0,3},{5,4},{6,5},{7,6},{4,7},{9,8},{10,9},{11,1... | collective-permute-start | bytes 405512 | tf_op jit(solution)/shard_map/ppermute | solution.py:267
  5.6 4.0 %collective-permute-start.2 = (f32[8,128]{1,0:T(8,128)S(1)}, f32[8,128]{1,0:T(8,128)S(1)}, u32[]{:S(2)}, u32[]{:S(2)}) collective-permute-start(f32[8,128]{1,0:T(8,128)S(1)} %get-tuple-element.17.mass), channel_id=1, source_target_pairs={{0,2},{1,3},{2,0},{3,1},{4,6},{5,7},{6,4},{7,5},{8,10},{9,11},{10,... | collective-permute-start | bytes 12296 | tf_op jit(solution)/shard_map/ppermute | solution.py:268
  10.3 17.3 %collective-permute-start.3 = (f32[8,10,8,128]{3,2,1,0:T(8,128)S(1)}, f32[8,10,8,128]{3,2,1,0:T(8,128)S(1)}, u32[]{:S(2)}, u32[]{:S(2)}) collective-permute-start(f32[8,10,8,128]{3,2,1,0:T(8,128)S(1)} %get-tuple-element.22), channel_id=1, source_target_pairs={{0,4},{4,8},{8,12},{12,16},{16,20},{20,24},{24,28},{28,32},{32,36}... | collective-permute-start | bytes 983048 | tf_op jit(solution)/shard_map/ppermute | solution.py:293
  14.0 13.6 %collective-permute-start.4 = (f32[8,10,8,128]{3,2,1,0:T(8,128)S(1)}, f32[8,10,8,128]{3,2,1,0:T(8,128)S(1)}, u32[]{:S(2)}, u32[]{:S(2)}) collective-permute-start(f32[8,10,8,128]{3,2,1,0:T(8,128)S(1)} %get-tuple-element.23), channel_id=1, source_target_pairs={{4,0},{8,4},{12,8},{16,12},{20,16},{24,20},{28,24},{32,28},{36,32}... | collective-permute-start | bytes 983048 | tf_op jit(solution)/shard_map/ppermute | solution.py:294
  14.2 22.0 %all-to-all-start = ((f32[64,1,128]{2,1,0:T(1,128)}), f32[64,1,128]{2,1,0:T(1,128)S(1)}, u32[]{:S(2)}, u32[]{:S(2)}) async-start(f32[64,1,128]{2,1,0:T(1,128)} %bitcast.3), calls=%async_computation | async-start | bytes 65536 | tf_op jit(solution)/shard_map/all_to_all | solution.py:295
